TPU v7x, 32 devices: a whole 2x2x4 slice. The times are simulated.
32 devices in a mesh: groups: 2 (over y), row: 4 (over z), head: 4 (over x, core).
Axes of the slice: x: 2, y: 2, z: 4, core: 2. Of those that a mesh axis runs over, the one named last changes fastest.
Arguments:
- tokens: bfloat16 [32, 2048], P('groups'), parts along dimension 0, may hold values from -6 to 6
- query_weight: bfloat16 [2048, 3072], P('row', 'head'), may hold values from -0.125 to 0.125
- latent_weight: bfloat16 [512, 4096], P('row', 'head'), may hold values from -0.25 to 0.25
- output_weight: bfloat16 [2048, 2048], P('row', 'head'), may hold values from -0.5 to 0.5
- cache_latent: bfloat16 [32, 2048, 512], P(('groups', 'row'), 'head'), parts along dimension 0, may hold values from -32 to 32
- cache_rope: bfloat16 [32, 64, 2048], P(('groups', 'row'), None, 'head'), parts along dimension 0, may hold values from -1800 to 1800
- lengths: int32 [32], P('groups'), parts along dimension 0, may hold values from 1 to 2048
- slot_seq: int32 [32], P('groups'), parts along dimension 0, may hold values from 0 to 15, each once
Outputs:
- attn_out: bfloat16 [32, 2048], P(('groups', 'row'), 'head'), parts along dimension 0
There are 2 independent parts, one for each index of `groups`. A program takes and returns all parts, laid end to end along the dimension named above; an argument that names none is the same for every part. Nothing has to cross between parts.
Inputs may be any that keep to these rules, and one draw needn't show every extreme that they name: Cache row i belongs to sequence slot_seq[i], and output row i is that sequence's. Positions at or past lengths[s] of a sequence hold stale entries that are not read; its new token stands at position lengths[s] - 1.
All inputs are finite; a program needn't handle non-finite values.
Results may differ from a plain program's by a relative error of at most 0.039.
Values may be sent and summed in bfloat16 or wider, within the bound.
A program may use at most 64 MiB of HBM per device.

v0:
```python
import jax
import jax.numpy as jnp
from jax import lax
from jax.sharding import PartitionSpec as P

D = 2048
H = 16
NOPE = 128
ROPE = 64
V = 128
LAT = 512
BLOCK = 256
neg_big = -1e30


def combined_all(part, axis, combine):
    gathered = jax.tree.map(lambda a: lax.all_gather(a, axis), part)

    def take(source):
        return jax.tree.map(lambda a: lax.dynamic_index_in_dim(a, source, 0, False), gathered)

    return lax.fori_loop(
        1, lax.axis_size(axis), lambda source, state: combine(state, take(source)), take(0)
    )


def absorb(query_weight, output_weight, kv_heads):
    width = query_weight.shape[0]
    head_total = kv_heads.shape[1]
    query_heads = query_weight.reshape(width, head_total, NOPE + ROPE)
    out_heads = output_weight.reshape(width, head_total, V)
    nope_part = jnp.einsum(
        "dhn,lhn->dhl",
        query_heads[:, :, :NOPE],
        kv_heads[:, :, :NOPE],
        preferred_element_type=jnp.float32,
    ).astype(jnp.bfloat16)
    query_abs = jnp.concatenate([nope_part, query_heads[:, :, NOPE:]], axis=2).reshape(width, -1)
    out_abs = jnp.einsum(
        "dhv,lhv->dhl", out_heads, kv_heads[:, :, NOPE:], preferred_element_type=jnp.float32
    ).astype(jnp.bfloat16)
    return (query_abs, out_abs.reshape(width, -1))


def rotate(queries, seq_len):
    half_width = ROPE // 2
    inverse_freq = jnp.power(10000.0, -2.0 * jnp.arange(half_width, dtype=jnp.float32) / ROPE)
    angles = (seq_len - 1).astype(jnp.float32)[:, None] * inverse_freq[None, :]
    cosine = jnp.cos(angles)[:, None, :]
    sine = jnp.sin(angles)[:, None, :]
    first_half = queries[:, :, LAT : LAT + half_width]
    second_half = queries[:, :, LAT + half_width :]
    rotated = jnp.concatenate(
        [first_half * cosine - second_half * sine, first_half * sine + second_half * cosine], axis=2
    )
    return jnp.concatenate([queries[:, :, :LAT], rotated], axis=2)


def combine(earlier, later):
    earlier_max, earlier_sum, earlier_acc = earlier
    later_max, later_sum, later_acc = later
    peak_max = jnp.maximum(earlier_max, later_max)
    earlier_scale = jnp.exp(earlier_max - peak_max)
    later_scale = jnp.exp(later_max - peak_max)
    summed = earlier_sum * earlier_scale + later_sum * later_scale
    weighted = earlier_acc * earlier_scale[..., None] + later_acc * later_scale[..., None]
    return (peak_max, summed, weighted)


def local(
    tokens, query_weight, latent_weight, output_weight, cache_latent, cache_rope, lengths, slot_seq
):
    heads_dev = query_weight.shape[1] // (NOPE + ROPE)
    seq_dev = cache_latent.shape[0]
    seg_len = cache_latent.shape[1]
    latent_full = lax.all_gather(latent_weight, "row", axis=0, tiled=True)
    kv_heads = latent_full.reshape(LAT, heads_dev, NOPE + V)
    full_query, full_out = (
        lax.all_gather(query_weight, "row", axis=0, tiled=True),
        lax.all_gather(output_weight, "row", axis=0, tiled=True),
    )
    query_abs, out_abs = absorb(full_query, full_out, kv_heads)
    first_row = lax.axis_index("row") * seq_dev
    seq_ids = lax.dynamic_slice_in_dim(slot_seq, first_row, seq_dev)
    chosen = tokens[seq_ids]
    seq_len = lengths[seq_ids]
    queries = jnp.dot(chosen, query_abs, preferred_element_type=jnp.float32).reshape(
        seq_dev, heads_dev, LAT + ROPE
    )
    queries = (
        rotate(queries, seq_len).astype(jnp.bfloat16).reshape(seq_dev, heads_dev * (LAT + ROPE))
    )
    queries = lax.all_gather(queries, "head", axis=1, tiled=True).reshape(seq_dev, H, LAT + ROPE)
    query_latent = queries[:, :, :LAT]
    query_rope = queries[:, :, LAT:]
    score_scale = 1.0 / jnp.sqrt(jnp.float32(NOPE + ROPE))
    offset = lax.axis_index("head") * seg_len
    local_len = jnp.clip(seq_len - offset, 0, seg_len)
    live_blocks = (jnp.max(local_len) + BLOCK - 1) // BLOCK

    def advance(block_idx, running):
        run_max, run_sum, run_acc = running
        begin_at = block_idx * BLOCK
        latent_blk = lax.dynamic_slice_in_dim(cache_latent, begin_at, BLOCK, 1)
        rope_blk = lax.dynamic_slice_in_dim(cache_rope, begin_at, BLOCK, 2)
        scores = jnp.einsum(
            "bhl,btl->bht", query_latent, latent_blk, preferred_element_type=jnp.float32
        )
        scores = (
            scores
            + jnp.einsum("bhr,brt->bht", query_rope, rope_blk, preferred_element_type=jnp.float32)
        ) * score_scale
        in_range = (begin_at + jnp.arange(BLOCK, dtype=jnp.int32))[None, None, :] < local_len[
            :, None, None
        ]
        masked = jnp.where(in_range, scores, neg_big)
        new_max = jnp.maximum(run_max, jnp.max(masked, axis=2))
        weights = jnp.where(in_range, jnp.exp(masked - new_max[..., None]), 0.0)
        factor = jnp.exp(run_max - new_max)
        run_sum = run_sum * factor + jnp.sum(weights, axis=2)
        run_acc = run_acc * factor[..., None] + jnp.einsum(
            "bht,btl->bhl",
            weights.astype(jnp.bfloat16),
            latent_blk,
            preferred_element_type=jnp.float32,
        )
        return (new_max, run_sum, run_acc)

    initial = (
        jnp.full((seq_dev, H), neg_big, jnp.float32),
        jnp.zeros((seq_dev, H), jnp.float32),
        jnp.zeros((seq_dev, H, LAT), jnp.float32),
    )
    partial_state = lax.fori_loop(0, live_blocks, advance, initial)
    merged_max, merged_sum, merged_acc = combined_all(partial_state, "head", combine)
    latent_out = (merged_acc / merged_sum[..., None]).astype(jnp.bfloat16)
    own_heads = lax.dynamic_slice_in_dim(
        latent_out, lax.axis_index("head") * heads_dev, heads_dev, 1
    )
    out_term = jnp.einsum(
        "bhl,dhl->bd",
        own_heads,
        out_abs.reshape(D, heads_dev, LAT),
        preferred_element_type=jnp.float32,
    )
    return lax.psum_scatter(out_term, "head", scatter_dimension=1, tiled=True).astype(jnp.bfloat16)


def solution(mesh):
    placed = (
        P("groups", None),
        P("row", "head"),
        P("row", "head"),
        P("row", "head"),
        P(("groups", "row"), "head", None),
        P(("groups", "row"), None, "head"),
        P("groups"),
        P("groups"),
    )
    return jax.shard_map(
        local, mesh=mesh, in_specs=placed, out_specs=P(("groups", "row"), "head"), check_vma=False
    )
```

profile of v0, /device:TPU:0, one launch (start us, length us, event | category | flops | bytes accessed | tf_op | source)
XLA Modules:
  0.0 190.2 jit_solution(7725425204575464518)
XLA Ops:
  6.5 0.0 copy-start
  6.5 0.0 all-gather.11.cloned.1.call-start
  6.5 2.3 %copy.30 = bf16[512,768]{0,1:T(8,128)(2,1)} copy(bf16[512,768]{1,0:T(8,128)(2,1)} %param.13) | data formatting | bytes 1572864 | tf_op args[1]
  8.9 0.0 all-gather.11.cloned.1.call-update
  8.9 0.0 all-gather.9.cloned.1.call-start
  9.0 1.8 copy.28
  10.8 0.0 all-gather.9.cloned.1.call-update
  10.8 0.0 all-gather.13.cloned.1.call-start
  10.8 2.0 %copy.36 = bf16[512,512]{0,1:T(8,128)(2,1)} copy(bf16[512,512]{1,0:T(8,128)(2,1)} %param.15) | data formatting | bytes 1048576 | tf_op args[3]
  12.9 0.0 all-gather.13.cloned.1.call-update
  12.9 0.0 reduce-scatter.4.cloned.1.call-start
  13.0 0.7 compare_select_fusion
  13.7 1.3 gather_fusion
  15.0 0.6 fusion.42
  16.3 0.0 copy-done
  16.3 0.6 gather_fusion.1
  16.9 0.1 multiply_cosine_fusion
  17.0 58.2 %all-gather.11.cloned.1.call-done = bf16[2048,768]{0,1:T(8,128)(2,1)} async-done(((bf16[512,768]{0,1:T(8,128)(2,1)}), bf16[2048,768]{0,1:T(8,128)(2,1)}) %all-gather.11.cloned.1.call-update) | async-done | bytes 3145744 | tf_op jit(solution)/shard_map/all_gather | solution.py:79
  75.2 2.3 %slice.51 = bf16[2048,4,64]{0,2,1:T(8,128)(2,1)} slice(bf16[2048,4,192]{0,2,1:T(8,128)(2,1)} %bitcast.61), slice={[0:2048], [0:4], [128:192]} | slice | bytes 2097152 | tf_op jit(solution)/shard_map/slice | solution.py:38
  77.5 27.8 %all-gather.9.cloned.1.call-done = bf16[512,1024]{0,1:T(8,128)(2,1)} async-done(((bf16[128,1024]{0,1:T(8,128)(2,1)}), bf16[512,1024]{0,1:T(8,128)(2,1)}) %all-gather.9.cloned.1.call-update) | async-done | bytes 1048592 | tf_op jit(solution)/shard_map/all_gather | solution.py:76
  105.4 0.0 copy-start.3
  105.4 4.2 %convert_bitcast_fusion = bf16[2048,4,512]{0,2,1:T(8,128)(2,1)S(1)} fusion(bf16[2048,4,192]{0,2,1:T(8,128)(2,1)} %bitcast.62, bf16[512,4,256]{0,2,1:T(8,128)(2,1)} %bitcast.64), kind=kOutput, calls=%fused_computation.40 | convolution fusion | flops 1077936128 | bytes 11010048 | tf_op jit(solution)/shard_map/dhn,lhn->dhl/dot_general | solution.py:32
  109.6 0.0 copy-done.3
  109.6 0.0 copy-start.1
  109.6 0.0 copy-start.2
  109.6 2.8 %fusion.20 = f32[4,4,576]{2,0,1:T(4,128)S(1)} fusion(bf16[2048,4,64]{0,2,1:T(8,128)(2,1)S(1)} %copy-done.3, bf16[2048,4,512]{0,2,1:T(8,128)(2,1)S(1)} %convert_bitcast_fusion, bf16[4,2048]{1,0:T(4,128)(2,1)S(1)} %gather_fusion.1), kind=kOutput, calls=%fused_computation.34 | convolution fusion | flops 56623104 | bytes 9490432 | tf_op jit(solution)/shard_map/dot_general | solution.py:87
  112.5 0.1 subtract_convert_fusion
  112.5 0.1 pad_maximum_fusion
  112.6 0.1 convert_element_type.36
  112.7 5.3 %all_gather.32 = bf16[4,9216]{1,0:T(4,128)(2,1)S(1)} all-gather(bf16[4,2304]{1,0:T(4,128)(2,1)S(1)} %convert_element_type.36), channel_id=1, replica_groups=mesh['groups'=2,'row'=4,'head'=4] {'head'}, dimensions={1}, use_global_device_ids=true | all-gather | bytes 92160 | tf_op jit(solution)/shard_map/all_gather | solution.py:93
  118.0 0.1 reshape.117
  118.2 0.0 copy-done.1
  118.2 0.0 copy-done.2
  118.2 2.4 %while.33 = (s32[]{:T(128)}, f32[4,16]{1,0:T(4,128)S(1)}, f32[4,16]{1,0:T(4,128)S(1)}, f32[4,16,512]{2,1,0:T(8,128)S(1)}, s32[]{:T(128)}, /*index=5*/s32[4]{0:T(...) while((s32[]{:T(128)}, f32[4,16]{1,0:T(4,128)S(1)}, ...), condition=%wide.region_4.5_spmd, body=%wide.region_1.4_spmd.sunk | while | flops 35882372 | bytes 2914003 | solution.py:134
  118.2 0.4 fusion.62
  118.6 0.1 broadcast_compare_fusion.2
  118.7 0.2 fusion.63
  119.0 0.2 fusion.64
  119.1 0.3 convolution_add_fusion.3
  119.5 0.4 fusion.62
  119.8 0.1 broadcast_compare_fusion.2
  119.9 0.2 fusion.63
  120.2 0.2 fusion.64
  120.3 0.3 convolution_add_fusion.3
  120.6 7.3 %all-gather.2 = f32[16,16,512]{2,1,0:T(8,128)S(1)} all-gather(f32[4,16,512]{2,1,0:T(8,128)S(1)} %get-tuple-element.239), channel_id=4, replica_groups=mesh['groups'=2,'row'=4,'head'=4] {'head'}, dimensions={0}, use_global_device_ids=true | all-gather | bytes 655360 | tf_op jit(solution)/shard_map/all_gather | solution.py:17
  127.9 5.2 %all-gather.4 = f32[4,4,16]{2,1,0:T(4,128)S(1)} all-gather(f32[1,4,16]{2,1,0:T(4,128)S(1)} %bitcast.68), channel_id=3, replica_groups=mesh['groups'=2,'row'=4,'head'=4] {'head'}, dimensions={0}, use_global_device_ids=true | all-gather | bytes 1280 | tf_op jit(solution)/shard_map/all_gather | solution.py:17
  133.1 5.2 %all-gather.3 = f32[4,4,16]{2,1,0:T(4,128)S(1)} all-gather(f32[1,4,16]{2,1,0:T(4,128)S(1)} %bitcast.66), channel_id=2, replica_groups=mesh['groups'=2,'row'=4,'head'=4] {'head'}, dimensions={0}, use_global_device_ids=true | all-gather | bytes 1280 | tf_op jit(solution)/shard_map/all_gather | solution.py:17
  138.3 0.4 while.34
  138.3 0.1 fusion.66
  138.5 0.1 fusion.66
  138.6 0.1 fusion.66
  138.7 0.1 copy.34
  138.8 0.1 copy.33
  138.9 12.0 %all-gather.13.cloned.1.call-done = bf16[2048,512]{0,1:T(8,128)(2,1)} async-done(((bf16[512,512]{0,1:T(8,128)(2,1)}), bf16[2048,512]{0,1:T(8,128)(2,1)}) %all-gather.13.cloned.1.call-update) | async-done | bytes 2097168 | tf_op jit(solution)/shard_map/all_gather | solution.py:80
  151.0 7.3 %fusion.28 = f32[2048,4]{1,0:T(8,128)} fusion(bf16[2048,4,128]{0,2,1:T(8,128)(2,1)} %bitcast.69, bf16[512,4,256]{0,2,1:T(8,128)(2,1)} %bitcast.65, f32[4,16,512]{2,0,1:T(4,128)S(1)} %copy.34, s32[]{:T(128)S(6)} %select_n.49, f32[4,4]{0,1:T(4,128)S(1)} %constant_dynamic-slice_fusion), kind=kOutput, calls=%fused_computation.42 | convolution fusion | flops 1111506944 | bytes 2689028 | tf_op jit(solution)/shard_map/bhl,dhl->bd/dot_general | solution.py:140
  158.3 0.0 reduce-scatter.4.cloned.1.call-update
  158.3 23.7 %reduce-scatter.4.cloned.1.call-done = f32[512,4]{1,0:T(8,128)} async-done(((f32[2048,4]{1,0:T(8,128)}), f32[512,4]{1,0:T(8,128)}) %reduce-scatter.4.cloned.1.call-update) | async-done | bytes 8208
  182.0 1.7 copy.42
  (24 shorter events, 0.2 us)
Async XLA Ops:
  6.5 9.8 %copy-start = (bf16[16,2048]{1,0:T(8,128)(2,1)S(1)}, bf16[16,2048]{1,0:T(8,128)(2,1)}, u32[]{:S(2)}) copy-start(bf16[16,2048]{1,0:T(8,128)(2,1)} %param.12) | copy-start | bytes 196612
  6.5 68.7 %all-gather.11.cloned.1.call-start = ((), (), s32[]{:S(2)}) async-start(), calls=%async_computation.2 | async-start | bytes 3932160 | tf_op jit(solution)/shard_map/all_gather | solution.py:79
  8.9 96.5 %all-gather.9.cloned.1.call-start = ((), (), s32[]{:S(2)}) async-start(), calls=%async_computation.1 | async-start | bytes 1310720 | tf_op jit(solution)/shard_map/all_gather | solution.py:76
  10.8 140.2 %all-gather.13.cloned.1.call-start = ((), (), s32[]{:S(2)}) async-start(), calls=%async_computation.3 | async-start | bytes 2621440 | tf_op jit(solution)/shard_map/all_gather | solution.py:80
  12.9 169.1 %reduce-scatter.4.cloned.1.call-start = ((), (), s32[]{:S(2)}) async-start(), calls=%async_computation.4 | async-start | bytes 1310720
  105.4 4.2 %copy-start.3 = (bf16[2048,4,64]{0,2,1:T(8,128)(2,1)S(1)}, bf16[2048,4,64]{0,2,1:T(8,128)(2,1)}, u32[]{:S(2)}) copy-start(bf16[2048,4,64]{0,2,1:T(8,128)(2,1)} %slice.51) | copy-start | bytes 3145732
  109.6 8.6 %copy-start.1 = (bf16[4,512,512]{2,1,0:T(8,128)(2,1)S(1)}, bf16[4,512,512]{2,1,0:T(8,128)(2,1)}, u32[]{:S(2)}) copy-start(bf16[4,512,512]{2,1,0:T(8,128)(2,1)} %param.16) | copy-start | bytes 6291460
  109.6 8.6 %copy-start.2 = (bf16[4,64,512]{2,1,0:T(8,128)(2,1)S(1)}, bf16[4,64,512]{2,1,0:T(8,128)(2,1)}, u32[]{:S(2)}) copy-start(bf16[4,64,512]{2,1,0:T(8,128)(2,1)} %param.17) | copy-start | bytes 786436
Sparse Core Ops, SparseCore 0:
  9.0 66.1 all-gather.10
  76.8 28.5 all-gather.8
  107.0 43.9 all-gather.12
  158.4 23.5 reduce-scatter.3
where the time goes:
time: 191 us; the launch traced here: 190 us
  waiting for transfers between devices  122 us (64%)
  blocking collectives  22.9 us (12%)
  matrix products  16.1 us (8%)
  between operations  14 us (7%)
  local copies, waits for them, and re-layouts  12.5 us (7%)
  other arithmetic  2.54 us (1%)
    all_gather x1, waiting for transfers between devices, local(): lax.all_gather(query_weight, 'row', axis=0, tiled=True)  58.2 us
    all_gather x1, waiting for transfers between devices, local(): latent_full = lax.all_gather(latent_weight, 'row', axis=0, tiled=True)  27.8 us
    unnamed x5, waiting for transfers between devices  23.8 us
    all_gather x3, blocking collectives, combined_all(): gathered = jax.tree.map(lambda a: lax.all_gather(a, axis), part)  17.6 us
    all_gather x1, waiting for transfers between devices, local(): lax.all_gather(output_weight, 'row', axis=0, tiled=True)  12 us
    unnamed x12, local copies, waits for them, and re-layouts  7.88 us
    dot_general x1, matrix products, local(): jnp.einsum('bhl,dhl->bd', own_heads, out_abs.reshape(D, heads_dev, LAT),...  7.3 us
    all_gather x1, blocking collectives, local(): lax.all_gather(queries, 'head', axis=1, tiled=True)  5.26 us
  transfers between devices with their start and end apart: 4, of which 4 were waited for; matrix products, arithmetic and copies ran while one was open for 10% of the time, Pallas kernels for 0%

commit v1 on v0

--- a/solution.py
+++ b/solution.py
@@ -73,7 +73,12 @@
     heads_dev = query_weight.shape[1] // (NOPE + ROPE)
     seq_dev = cache_latent.shape[0]
     seg_len = cache_latent.shape[1]
-    latent_full = lax.all_gather(latent_weight, "row", axis=0, tiled=True)
+    ring = [latent_weight]
+    for hop in range(3):
+        ring.append(lax.ppermute(ring[-1], "row", [(dev, (dev + 1) % 4) for dev in range(4)]))
+    latent_full = jnp.roll(
+        jnp.concatenate(ring[::-1], axis=0), (lax.axis_index("row") + 1) * ring[0].shape[0], axis=0
+    )
     kv_heads = latent_full.reshape(LAT, heads_dev, NOPE + V)
     full_query, full_out = (
         lax.all_gather(query_weight, "row", axis=0, tiled=True),

time: 191 us -> 172 us (0.901)
  waiting for transfers between devices: 122 us -> 101 us
  starting transfers between devices: 0.13 us -> 4.29 us
  local copies, waits for them, and re-layouts: 12.5 us -> 9.04 us
    ppermute x0 -> x3, waiting for transfers between devices: none -> 36.6 us  [local(): lax.ppermute(ring[-1], 'row', [(dev, (dev + 1) % 4) for dev in range(4)])]
    all_gather x1 -> x0, waiting for transfers between devices: 27.8 us -> none  [local(): latent_full = lax.all_gather(latent_weight, 'row', axis=0, tiled=True)]
    all_gather x1, waiting for transfers between devices: 58.2 us -> 31.6 us  [local(): lax.all_gather(query_weight, 'row', axis=0, tiled=True)]
    ppermute x0 -> x3, starting transfers between devices: none -> 4.17 us  [local(): lax.ppermute(ring[-1], 'row', [(dev, (dev + 1) % 4) for dev in range(4)])]
    all_gather x1, waiting for transfers between devices: 12 us -> 9.38 us  [local(): lax.all_gather(output_weight, 'row', axis=0, tiled=True)]
    unnamed x12 -> x23, local copies, waits for them, and re-layouts: 7.88 us -> 5.86 us
    unnamed x5 -> x4, waiting for transfers between devices: 23.8 us -> 23.8 us
  transfers between devices with their start and end apart: 4 -> 6, of which waited for: 4 -> 6; matrix products, arithmetic and copies ran while one was open for 10% -> 10% of each run, Pallas kernels for 0% -> 0%
where the time goes in v1:
time: 172 us; the launch traced here: 171 us
  waiting for transfers between devices  101 us (59%)
  blocking collectives  22.9 us (13%)
  matrix products  17.5 us (10%)
  between operations  14.1 us (8%)
  local copies, waits for them, and re-layouts  9.04 us (5%)
  starting transfers between devices  4.29 us (2%)
  other arithmetic  1.89 us (1%)
    ppermute x3, waiting for transfers between devices, local(): lax.ppermute(ring[-1], 'row', [(dev, (dev + 1) % 4) for dev in range(4)])  36.6 us
    all_gather x1, waiting for transfers between devices, local(): lax.all_gather(query_weight, 'row', axis=0, tiled=True)  31.6 us
    unnamed x4, waiting for transfers between devices  23.8 us
    all_gather x3, blocking collectives, combined_all(): gathered = jax.tree.map(lambda a: lax.all_gather(a, axis), part)  17.6 us
    all_gather x1, waiting for transfers between devices, local(): lax.all_gather(output_weight, 'row', axis=0, tiled=True)  9.38 us
    dot_general x1, matrix products, local(): jnp.einsum('bhl,dhl->bd', own_heads, out_abs.reshape(D, heads_dev, LAT),...  7.13 us
    unnamed x23, local copies, waits for them, and re-layouts  5.86 us
    all_gather x1, blocking collectives, local(): lax.all_gather(queries, 'head', axis=1, tiled=True)  5.26 us
  transfers between devices with their start and end apart: 6, of which 6 were waited for; matrix products, arithmetic and copies ran while one was open for 10% of the time, Pallas kernels for 0%

profile of v1, /device:TPU:0, one launch (start us, length us, event | category | flops | bytes accessed | tf_op | source)
XLA Modules:
  0.0 171.2 jit_solution(37791818982334649)
XLA Ops:
  6.5 0.0 all-gather.8.cloned.1.call-start
  6.6 2.4 %copy.36 = bf16[512,768]{0,1:T(8,128)(2,1)} copy(bf16[512,768]{1,0:T(8,128)(2,1)} %param.13) | data formatting | bytes 1572864 | tf_op args[1]
  9.0 0.0 all-gather.8.cloned.1.call-update
  9.0 0.0 all-gather.10.cloned.1.call-start
  9.1 0.2 copy.32
  9.3 3.1 %collective-permute-start = (bf16[128,1024]{0,1:T(8,128)(2,1)S(1)}, bf16[128,1024]{0,1:T(8,128)(2,1)S(1)}, u32[]{:S(2)}, u32[]{:S(2)}) collective-permute-start(bf16[128,1024]{0,1:T(8,128)(2,1)S(1)} %copy.32), channel_id=1, source_target_pairs={{0,4},{4,8},{8,12},{12,0},{1,5},{5,9},{9,13},{13,1},{2,6},{6,10},{... | collective-permute-start | bytes 786440 | tf_op jit(solution)/shard_map/ppermute | solution.py:78
  12.4 1.0 copy.42
  13.4 0.0 all-gather.10.cloned.1.call-update
  13.4 0.0 reduce-scatter.4.cloned.1.call-start
  13.5 0.1 compare_select_fusion
  13.6 7.1 %collective-permute-done = bf16[128,1024]{0,1:T(8,128)(2,1)S(1)} collective-permute-done((bf16[128,1024]{0,1:T(8,128)(2,1)S(1)}, bf16[128,1024]{0,1:T(8,128)(2,1)S(1)}, u32[]{:S(2)}, u32[]{:S(2)}) %collective-permute-start) | collective-permute-done | bytes 262176 | tf_op jit(solution)/shard_map/ppermute | solution.py:78
  20.7 0.0 collective-permute-start.1
  20.7 0.6 gather_fusion
  21.4 0.6 fusion.42
  22.0 14.7 %collective-permute-done.1 = bf16[128,1024]{0,1:T(8,128)(2,1)S(1)} collective-permute-done((bf16[128,1024]{0,1:T(8,128)(2,1)S(1)}, bf16[128,1024]{0,1:T(8,128)(2,1)S(1)}, u32[]{:S(2)}, u32[]{:S(2)}) %collective-permute-start.1) | collective-permute-done | bytes 262176 | tf_op jit(solution)/shard_map/ppermute | solution.py:78
  36.7 1.1 collective-permute-start.2
  38.4 0.6 gather_fusion.1
  39.0 0.1 multiply_cosine_fusion
  39.1 14.8 %collective-permute-done.2 = bf16[128,1024]{0,1:T(8,128)(2,1)S(1)} collective-permute-done((bf16[128,1024]{0,1:T(8,128)(2,1)S(1)}, bf16[128,1024]{0,1:T(8,128)(2,1)S(1)}, u32[]{:S(2)}, u32[]{:S(2)}) %collective-permute-start.2) | collective-permute-done | bytes 262176 | tf_op jit(solution)/shard_map/ppermute | solution.py:78
  53.9 0.1 constant_dynamic-update-slice_fusion.7
  54.0 0.1 constant_dynamic-update-slice_fusion.6
  54.1 0.1 constant_dynamic-update-slice_fusion.5
  54.2 0.1 constant_dynamic-update-slice_fusion.4
  54.3 0.1 constant_dynamic-update-slice_fusion.3
  54.4 0.1 constant_dynamic-update-slice_fusion.2
  54.5 0.1 constant_dynamic-update-slice_fusion.1
  54.6 0.1 constant_dynamic-update-slice_fusion
  54.7 0.1 constant_dynamic-slice_fusion.1
  54.8 31.6 %all-gather.8.cloned.1.call-done = bf16[2048,768]{0,1:T(8,128)(2,1)} async-done(((bf16[512,768]{0,1:T(8,128)(2,1)}), bf16[2048,768]{0,1:T(8,128)(2,1)}) %all-gather.8.cloned.1.call-update) | async-done | bytes 3145744 | tf_op jit(solution)/shard_map/all_gather | solution.py:84
  86.4 1.3 slice.51
  87.7 4.0 %convert_bitcast_fusion = bf16[2048,4,512]{0,2,1:T(8,128)(2,1)S(1)} fusion(bf16[2048,4,192]{0,2,1:T(8,128)(2,1)} %bitcast.62, bf16[512,4,256]{0,2,1:T(8,128)(2,1)S(1)} %bitcast.64), kind=kOutput, calls=%fused_computation.40 | convolution fusion | flops 1077936128 | bytes 11010048 | tf_op jit(solution)/shard_map/dhn,lhn->dhl/dot_general | solution.py:32
  91.7 0.0 copy-start.2
  91.7 2.8 %fusion.20 = f32[4,4,576]{2,0,1:T(4,128)S(1)} fusion(bf16[2048,4,64]{0,2,1:T(8,128)(2,1)S(1)} %slice.51, bf16[2048,4,512]{0,2,1:T(8,128)(2,1)S(1)} %convert_bitcast_fusion, bf16[4,2048]{1,0:T(4,128)(2,1)S(1)} %gather_fusion.1), kind=kOutput, calls=%fused_computation.34 | convolution fusion | flops 56623104 | bytes 9490432 | tf_op jit(solution)/shard_map/dot_general | solution.py:92
  94.5 0.1 subtract_convert_fusion
  94.6 0.1 pad_maximum_fusion
  94.7 0.1 convert_element_type.36
  94.8 5.3 %all_gather.28 = bf16[4,9216]{1,0:T(4,128)(2,1)S(1)} all-gather(bf16[4,2304]{1,0:T(4,128)(2,1)S(1)} %convert_element_type.36), channel_id=1, replica_groups=mesh['groups'=2,'row'=4,'head'=4] {'head'}, dimensions={1}, use_global_device_ids=true | all-gather | bytes 92160 | tf_op jit(solution)/shard_map/all_gather | solution.py:98
  100.0 0.1 reshape.117
  100.2 0.0 copy-done.2
  100.3 4.2 %while.33 = (s32[]{:T(128)}, f32[4,16]{1,0:T(4,128)S(1)}, f32[4,16]{1,0:T(4,128)S(1)}, f32[4,16,512]{2,1,0:T(8,128)S(1)}, s32[]{:T(128)}, /*index=5*/s32[4]{0:T(...) while((s32[]{:T(128)}, f32[4,16]{1,0:T(4,128)S(1)}, ...), condition=%wide.region_4.5_spmd, body=%wide.region_1.4_spmd.sunk | while | flops 35882372 | bytes 2905811 | solution.py:139
  100.3 0.4 fusion.62
  100.7 0.1 broadcast_compare_fusion.2
  100.7 1.1 fusion.63
  101.9 0.2 fusion.64
  102.1 0.3 convolution_add_fusion.3
  102.4 0.4 fusion.62
  102.8 0.1 broadcast_compare_fusion.2
  102.8 1.1 fusion.63
  104.0 0.2 fusion.64
  104.2 0.3 convolution_add_fusion.3
  104.5 7.3 %all-gather.2 = f32[16,16,512]{2,1,0:T(8,128)S(1)} all-gather(f32[4,16,512]{2,1,0:T(8,128)S(1)} %get-tuple-element.239), channel_id=4, replica_groups=mesh['groups'=2,'row'=4,'head'=4] {'head'}, dimensions={0}, use_global_device_ids=true | all-gather | bytes 655360 | tf_op jit(solution)/shard_map/all_gather | solution.py:17
  111.8 5.2 %all-gather.4 = f32[4,4,16]{2,1,0:T(4,128)S(1)} all-gather(f32[1,4,16]{2,1,0:T(4,128)S(1)} %bitcast.68), channel_id=3, replica_groups=mesh['groups'=2,'row'=4,'head'=4] {'head'}, dimensions={0}, use_global_device_ids=true | all-gather | bytes 1280 | tf_op jit(solution)/shard_map/all_gather | solution.py:17
  117.0 5.2 %all-gather.3 = f32[4,4,16]{2,1,0:T(4,128)S(1)} all-gather(f32[1,4,16]{2,1,0:T(4,128)S(1)} %bitcast.66), channel_id=2, replica_groups=mesh['groups'=2,'row'=4,'head'=4] {'head'}, dimensions={0}, use_global_device_ids=true | all-gather | bytes 1280 | tf_op jit(solution)/shard_map/all_gather | solution.py:17
  122.1 0.4 while.34
  122.2 0.1 fusion.66
  122.3 0.1 fusion.66
  122.5 0.1 fusion.66
  122.6 0.1 copy.40
  122.7 0.1 copy.39
  122.8 9.4 %all-gather.10.cloned.1.call-done = bf16[2048,512]{0,1:T(8,128)(2,1)} async-done(((bf16[512,512]{0,1:T(8,128)(2,1)}), bf16[2048,512]{0,1:T(8,128)(2,1)}) %all-gather.10.cloned.1.call-update) | async-done | bytes 2097168 | tf_op jit(solution)/shard_map/all_gather | solution.py:85
  132.1 7.1 %fusion.28 = f32[2048,4]{1,0:T(8,128)} fusion(bf16[2048,4,128]{0,2,1:T(8,128)(2,1)} %bitcast.69, bf16[512,4,256]{0,2,1:T(8,128)(2,1)S(1)} %bitcast.65, f32[4,16,512]{2,0,1:T(4,128)S(1)} %copy.40, s32[]{:T(128)S(6)} %select_n.63, f32[4,4]{0,1:T(4,128)S(1)} %constant_dynamic-slice_fusion), kind=kOutput, calls=%fused_computation.42 | convolution fusion | flops 1111506944 | bytes 2689028 | tf_op jit(solution)/shard_map/bhl,dhl->bd/dot_general | solution.py:145
  139.3 0.0 reduce-scatter.4.cloned.1.call-update
  139.3 23.7 %reduce-scatter.4.cloned.1.call-done = f32[512,4]{1,0:T(8,128)} async-done(((f32[2048,4]{1,0:T(8,128)}), f32[512,4]{1,0:T(8,128)}) %reduce-scatter.4.cloned.1.call-update) | async-done | bytes 8208
  163.0 1.7 copy.48
  (34 shorter events, 0.2 us)
Async XLA Ops:
  6.5 31.9 %copy-start = (bf16[16,2048]{1,0:T(8,128)(2,1)S(1)}, bf16[16,2048]{1,0:T(8,128)(2,1)}, u32[]{:S(2)}) copy-start(bf16[16,2048]{1,0:T(8,128)(2,1)} %param.12) | copy-start | bytes 196612
  6.5 2.5 %copy-start.4 = (bf16[128,1024]{1,0:T(8,128)(2,1)S(1)}, bf16[128,1024]{1,0:T(8,128)(2,1)}, u32[]{:S(2)}) copy-start(bf16[128,1024]{1,0:T(8,128)(2,1)} %param.14) | copy-start | bytes 786436
  6.5 5.8 %copy-start.3 = (bf16[512,512]{1,0:T(8,128)(2,1)S(1)}, bf16[512,512]{1,0:T(8,128)(2,1)}, u32[]{:S(2)}) copy-start(bf16[512,512]{1,0:T(8,128)(2,1)} %param.15) | copy-start | bytes 1572868
  6.5 6.9 %copy-start.5 = (s32[16]{0:T(128)S(1)}, s32[16]{0:T(128)}, u32[]{:S(2)}) copy-start(s32[16]{0:T(128)} %param.19) | copy-start | bytes 196
  6.5 14.2 %copy-start.1 = (s32[16]{0:T(128)S(1)}, s32[16]{0:T(128)}, u32[]{:S(2)}) copy-start(s32[16]{0:T(128)} %param.18) | copy-start | bytes 196
  6.5 79.9 %all-gather.8.cloned.1.call-start = ((), (), s32[]{:S(2)}) async-start(), calls=%async_computation.1 | async-start | bytes 3932160 | tf_op jit(solution)/shard_map/all_gather | solution.py:84
  9.0 123.1 %all-gather.10.cloned.1.call-start = ((), (), s32[]{:S(2)}) async-start(), calls=%async_computation.2 | async-start | bytes 2621440 | tf_op jit(solution)/shard_map/all_gather | solution.py:85
  9.3 11.4 %collective-permute-start = (bf16[128,1024]{0,1:T(8,128)(2,1)S(1)}, bf16[128,1024]{0,1:T(8,128)(2,1)S(1)}, u32[]{:S(2)}, u32[]{:S(2)}) collective-permute-start(bf16[128,1024]{0,1:T(8,128)(2,1)S(1)} %copy.32), channel_id=1, source_target_pairs={{0,4},{4,8},{8,12},{12,0},{1,5},{5,9},{9,13},{13,1},{2,6},{6,10},{... | collective-permute-start | bytes 786440 | tf_op jit(solution)/shard_map/ppermute | solution.py:78
  13.4 149.6 %reduce-scatter.4.cloned.1.call-start = ((), (), s32[]{:S(2)}) async-start(), calls=%async_computation.3 | async-start | bytes 1310720
  20.7 16.0 %collective-permute-start.1 = (bf16[128,1024]{0,1:T(8,128)(2,1)S(1)}, bf16[128,1024]{0,1:T(8,128)(2,1)S(1)}, u32[]{:S(2)}, u32[]{:S(2)}) collective-permute-start(bf16[128,1024]{0,1:T(8,128)(2,1)S(1)} %collective-permute-done), channel_id=1, source_target_pairs={{0,4},{4,8},{8,12},{12,0},{1,5},{5,9},{9,13},{13,1},{2,6},{6,10},{... | collective-permute-start | bytes 786440 | tf_op jit(solution)/shard_map/ppermute | solution.py:78
  36.7 17.3 %collective-permute-start.2 = (bf16[128,1024]{0,1:T(8,128)(2,1)S(1)}, bf16[128,1024]{0,1:T(8,128)(2,1)S(1)}, u32[]{:S(2)}, u32[]{:S(2)}) collective-permute-start(bf16[128,1024]{0,1:T(8,128)(2,1)S(1)} %collective-permute-done.1), channel_id=1, source_target_pairs={{0,4},{4,8},{8,12},{12,0},{1,5},{5,9},{9,13},{13,1},{2,6},{6,10},{... | collective-permute-start | bytes 786440 | tf_op jit(solution)/shard_map/ppermute | solution.py:78
  91.7 8.6 %copy-start.2 = (bf16[4,512,512]{2,1,0:T(8,128)(2,1)S(1)}, bf16[4,512,512]{2,1,0:T(8,128)(2,1)}, u32[]{:S(2)}) copy-start(bf16[4,512,512]{2,1,0:T(8,128)(2,1)} %param.16) | copy-start | bytes 6291460
Sparse Core Ops, SparseCore 0:
  9.1 77.2 all-gather.7
  88.0 44.1 all-gather.9
  139.4 23.5 reduce-scatter.3
